TPU v7x, 256 devices: a whole 4x4x8 slice. The times are simulated.
256 devices in a mesh: role: 2 (over z_hi), dp: 16 (over y, z_lo), mp: 8 (over x, core).
Axes of the slice: x: 4, y: 4, z: 8 (z_hi: 2, z_lo: 4; z = z_hi * 4 + z_lo), core: 2. Of those that a mesh axis runs over, the one named last changes fastest.
Arguments:
- patches: bfloat16 [25088, 1280], P('dp', 'mp'), may hold values from -6 to 6
- pred_states: bfloat16 [16384, 384], P('dp'), may hold values from -6 to 6
- ema_up: bfloat16 [1280, 5120], P(('role', 'dp'), 'mp'), may hold values from -0.15625 to 0.15625
- ema_down: bfloat16 [5120, 1280], P('mp', ('role', 'dp')), may hold values from -0.078125 to 0.078125
- pred_up: bfloat16 [384, 1536], P(('role', 'dp'), 'mp'), may hold values from -0.3125 to 0.3125
- pred_down: bfloat16 [1536, 384], P('mp', ('role', 'dp')), may hold values from -0.15625 to 0.15625
- pred_out: bfloat16 [384, 1280], P(('role', 'dp'), 'mp'), may hold values from -0.3125 to 0.3125
- masked_index: int32 [16, 1024], P('dp'), may hold values from 0 to 1567, as said below
- masked_count: int32 [16], P('dp'), may hold values from 512 to 1024, as said below
- loss_scale: float32 [], replicated, may hold values from 81920 to 327680
Outputs:
- loss: float32 [], replicated
- grad_up: float32 [384, 1536], P(('role', 'dp'), 'mp')
- grad_down: float32 [1536, 384], P('mp', ('role', 'dp'))
- grad_out: float32 [384, 1280], P(('role', 'dp'), 'mp')
Inputs may be any that keep to these rules, and one draw needn't show every extreme that they name: `masked_index`: within a clip the slots name distinct tokens; the slots below masked_count name the masked tokens, which are whole tubes: all 8 frames (token f * 196 + s for frame f) of some spatial positions s. Slots from masked_count on name other tokens and are ignored. `masked_count`: each count is 8 times a whole number; some clip has exactly 1024.
All inputs are finite; a program needn't handle non-finite values.
Results may differ from a plain program's by a relative error of at most 0.012.
Values may be sent and summed in bfloat16 or wider, within the bound.
No kernel may reach another device: no remote copies, remote signals or barrier semaphores. Data moves between devices by JAX's collectives and lax.ppermute only.
A program may use at most 128 MiB of HBM per device.

v0:
```python
import functools
import jax
import jax.numpy as jnp
from jax import lax
from jax.sharding import Mesh
from jax.sharding import PartitionSpec as P

D = 1280
TOK = 1568
MMAX = 1024
MP = ("mp_0", "mp_1")
ROLE_DP = ("role", "dp_0", "dp_1")
DP = ("dp_0", "dp_1")
ROLE_DP_MP = ("role", "dp_0", "dp_1", "mp_0", "mp_1")
EPS = 1e-06
COEF = 0.7978845608028654


def joined_along(pieces, dim):
    pieces = jnp.moveaxis(pieces, 0, dim)
    lengths = pieces.shape
    return pieces.reshape(*lengths[:dim], lengths[dim] * lengths[dim + 1], *lengths[dim + 2 :])


def from_everyone(shard, axis):
    copies = jnp.broadcast_to(shard, (lax.axis_size(axis), *shard.shape))
    return lax.all_to_all(copies, axis, split_axis=0, concat_axis=0, tiled=True)


def gather_directly(shard, axis, dim):
    return joined_along(from_everyone(shard, axis), dim)


def of_everyone(shard, axis):
    return from_everyone(shard, axis).sum(axis=0)


def in_one(arrays, axis):
    vector, at, outs = (jnp.concatenate([a.reshape(-1) for a in arrays]), 0, [])
    total = of_everyone(vector, axis)
    for a in arrays:
        outs.append(total[at : at + a.size].reshape(a.shape))
        at += a.size
    return tuple(outs)


def passed_along(block, axis, distance):
    devices = range(lax.axis_size(axis))
    route = [(i - distance, i) for i in devices if i - distance in devices]
    return lax.ppermute(block, axis, route)


def sent_together(arrays, axis, dim, along):
    widths = [a.shape[along] for a in arrays]
    both = jnp.concatenate(arrays, axis=along)
    filled = lax.all_gather(both, axis, axis=dim, tiled=True)
    return tuple(jnp.split(filled, [sum(widths[:k]) for k in range(1, len(widths))], axis=along))


def by_axis(shard, axes):
    return functools.reduce(lax.psum, axes, shard)


def filled_up(lines, devices):
    spare = -len(lines) % devices
    return jnp.pad(lines, [(0, spare)] + [(0, 0)] * (lines.ndim - 1))


def sum_by_parts(shard, axis):
    lines = shard.reshape(-1, *shard.shape[1:][-1:])
    own = lax.psum_scatter(
        filled_up(lines, lax.axis_size(axis)), axis, scatter_dimension=0, tiled=True
    )
    whole = lax.all_gather(own, axis).reshape(-1, *lines.shape[1:])
    return lax.slice_in_dim(whole, 0, len(lines)).reshape(shard.shape)


def cut_along(shard, dim, devices):
    before, after = (shard.shape[:dim], shard.shape[dim + 1 :])
    return jnp.moveaxis(shard.reshape(*before, devices, -1, *after), dim, 0)


def sum_together(arrays, axis, dims):
    devices = lax.axis_size(axis)
    pieces = [cut_along(a, dim, devices) for a, dim in zip(arrays, dims)]
    lines = jnp.concatenate([b.reshape(devices, -1) for b in pieces], axis=1)
    width = max(16, -(-lines.shape[1] // 1024) * 8)
    lines = jnp.pad(lines, ((0, 0), (0, width * 128 - lines.shape[1]))).reshape(-1, 128)
    vector, at, outs = (lax.psum_scatter(lines, axis, tiled=True).reshape(-1), 0, [])
    for b in pieces:
        part = b[0]
        outs.append(vector[at : at + part.size].reshape(part.shape))
        at += part.size
    return tuple(outs)


def summed_on_arrival(shard, axis, dim):
    pieces = cut_along(shard, dim, lax.axis_size(axis))
    arrived = lax.all_to_all(pieces, axis, split_axis=0, concat_axis=0, tiled=True)
    return arrived.sum(axis=0)


def normalize(values):
    row_mean = jnp.mean(values, axis=-1, keepdims=True)
    row_deviations = values - row_mean
    variance = jnp.mean(row_deviations * row_deviations, axis=-1, keepdims=True)
    return row_deviations * lax.rsqrt(variance + EPS)


def gelu_slope(values):
    inner = COEF * (values + 0.044715 * values * values * values)
    tangent = jnp.tanh(inner)
    return 0.5 * (1.0 + tangent) + 0.5 * values * (1.0 - tangent * tangent) * COEF * (
        1.0 + 3.0 * 0.044715 * values * values
    )


def pick_rows(source_table, token_index):
    clip_count = token_index.shape[0]
    slot_total = token_index.shape[1]
    clip_grid = source_table.reshape(clip_count, TOK, source_table.shape[1])
    onehot = (token_index[:, :, None] == jnp.arange(TOK, dtype=jnp.int32)[None, None, :]).astype(
        jnp.bfloat16
    )
    picked = jnp.einsum("ckt,ctw->ckw", onehot, clip_grid, preferred_element_type=jnp.float32)
    return picked.astype(jnp.bfloat16).reshape(clip_count * slot_total, source_table.shape[1])


def body(
    patches,
    pred_states,
    ema_up,
    ema_down,
    pred_up,
    pred_down,
    pred_out,
    masked_index,
    masked_count,
    loss_scale,
):
    role_index = lax.axis_index("role")
    clip_count = masked_index.shape[0]
    feat_width = float(D)
    half_slots = MMAX // 2
    half_index = lax.dynamic_slice_in_dim(masked_index, role_index * half_slots, half_slots, 1)
    own_rows = pick_rows(patches, half_index)
    whole_rows = gather_directly(own_rows, MP, 1)
    working = role_index >= 0
    block_rows = own_rows.shape[0]
    up_cols = lax.all_gather(ema_up, ROLE_DP, axis=0, tiled=True)
    down_rows = lax.all_gather(ema_down, ROLE_DP, axis=1, tiled=True)

    def encode_block():
        normed = normalize(whole_rows.astype(jnp.float32)).astype(jnp.bfloat16)
        hidden = jax.nn.gelu(
            jnp.dot(normed, up_cols, preferred_element_type=jnp.float32), approximate=True
        ).astype(jnp.bfloat16)
        return jnp.dot(hidden, down_rows, preferred_element_type=jnp.float32)

    def skip_block():
        return jnp.zeros((block_rows, whole_rows.shape[1]), jnp.float32)

    partial_sum = lax.cond(working, encode_block, skip_block)
    branch = lax.psum_scatter(partial_sum, MP, scatter_dimension=1, tiled=True)
    block_out = own_rows.astype(jnp.float32) + branch
    first_sum, second_sum = in_one(
        (
            jnp.sum(block_out, axis=-1, keepdims=True),
            jnp.sum(block_out * block_out, axis=-1, keepdims=True),
        ),
        MP,
    )
    row_mean = first_sum / feat_width
    row_deviations = block_out - row_mean
    variance = second_sum / feat_width - row_mean * row_mean
    target_all = (row_deviations * lax.rsqrt(variance + EPS)).astype(jnp.bfloat16)
    local_width = target_all.shape[1]
    earlier = passed_along(target_all, "role", 1)
    joined = jnp.concatenate(
        (
            earlier.reshape(clip_count, half_slots, local_width),
            target_all.reshape(clip_count, half_slots, local_width),
        ),
        axis=1,
    )
    targets = joined.reshape(clip_count * MMAX, local_width)
    up_rows, out_rows = sent_together((pred_up, pred_out), ROLE_DP, 0, 1)
    down_cols = gather_directly(pred_down, ROLE_DP, 1)
    total = of_everyone(jnp.sum(masked_count).astype(jnp.float32), DP)
    states = pred_states.astype(jnp.float32)
    pnormed = normalize(states).astype(jnp.bfloat16)
    preact = jnp.dot(pnormed, up_rows, preferred_element_type=jnp.float32)
    hid_act = jax.nn.gelu(preact, approximate=True).astype(jnp.bfloat16)
    mixer_out = lax.psum(jnp.dot(hid_act, down_cols, preferred_element_type=jnp.float32), MP)
    updated = states + mixer_out
    row_mean_p = jnp.mean(updated, axis=-1, keepdims=True)
    predictor_deviations = updated - row_mean_p
    reciprocal_spread = lax.rsqrt(
        jnp.mean(predictor_deviations * predictor_deviations, axis=-1, keepdims=True) + EPS
    )
    standardized_input = predictor_deviations * reciprocal_spread
    output_normalized = standardized_input.astype(jnp.bfloat16)
    predicted = jnp.dot(output_normalized, out_rows, preferred_element_type=jnp.float32)
    live_mask = (
        (jnp.arange(MMAX, dtype=jnp.int32)[None, :] < masked_count[:, None])
        .astype(jnp.float32)
        .reshape(clip_count * MMAX, 1)
    )
    predictor_side = (role_index == 1).astype(jnp.float32)
    norm_scale = total * feat_width
    residue = predicted - targets.astype(jnp.float32)
    smooth = jnp.sqrt(residue * residue + 1.0)
    local_loss = jnp.sum(live_mask * (smooth - 1.0)) * predictor_side
    loss = by_axis(local_loss, ROLE_DP_MP) / norm_scale
    grad_pred = (loss_scale * live_mask * residue / smooth / norm_scale * predictor_side).astype(
        jnp.bfloat16
    )
    normalized_gradient = sum_by_parts(
        jnp.einsum("rd,kd->rk", grad_pred, out_rows, preferred_element_type=jnp.float32), MP
    )
    gradient_update = reciprocal_spread * (
        normalized_gradient
        - jnp.mean(normalized_gradient, axis=-1, keepdims=True)
        - standardized_input
        * jnp.mean(normalized_gradient * standardized_input, axis=-1, keepdims=True)
    )
    gradient_update = gradient_update.astype(jnp.bfloat16)
    down_local = jnp.einsum(
        "rf,rk->fk", hid_act, gradient_update, preferred_element_type=jnp.float32
    )
    grad_act = jnp.einsum(
        "rk,fk->rf", gradient_update, down_cols, preferred_element_type=jnp.float32
    )
    grad_pre = (grad_act * gelu_slope(preact)).astype(jnp.bfloat16)
    up_local = jnp.einsum("rk,rf->kf", pnormed, grad_pre, preferred_element_type=jnp.float32)
    out_local = jnp.einsum(
        "rk,rd->kd", output_normalized, grad_pred, preferred_element_type=jnp.float32
    )
    grad_up, grad_out = tuple(
        (
            part.astype(jnp.float32)
            for part in sum_together(
                (up_local.astype(jnp.bfloat16), out_local.astype(jnp.bfloat16)), ROLE_DP, (0, 0)
            )
        )
    )
    grad_down = summed_on_arrival(down_local, ROLE_DP, 1)
    return (loss, grad_up, grad_down, grad_out)


def solution(mesh):
    finer = Mesh(
        mesh.devices.reshape(mesh.shape["role"], 4, 4, 4, 2),
        ("role", "dp_0", "dp_1", "mp_0", "mp_1"),
    )
    return jax.shard_map(
        body,
        mesh=finer,
        in_specs=(
            P(DP, MP),
            P(DP, None),
            P(ROLE_DP, MP),
            P(MP, ROLE_DP),
            P(ROLE_DP, MP),
            P(MP, ROLE_DP),
            P(ROLE_DP, MP),
            P(DP, None),
            P(DP),
            P(),
        ),
        out_specs=(P(), P(ROLE_DP, MP), P(MP, ROLE_DP), P(ROLE_DP, MP)),
        check_vma=False,
    )
```

profile of v0, /device:TPU:2, one launch (start us, length us, event | category | flops | bytes accessed | tf_op | source)
XLA Modules:
  0.0 619.0 jit_solution(12182839815354292576)
XLA Ops:
  10.9 11.5 %all-to-all-start = ((bf16[32,192,12]{1,2,0:T(8,128)(2,1)}), bf16[32,192,12]{1,2,0:T(8,128)(2,1)S(1)}, u32[]{:S(2)}, u32[]{:S(2)}) async-start(bf16[32,192,12]{1,2,0:T(8,128)(2,1)} %broadcast_in_dim.10), calls=%async_computation | async-start | bytes 524288 | tf_op jit(solution)/shard_map/all_to_all | solution.py:27
  23.2 75.8 %all-gather.1 = bf16[32,12,352]{2,1,0:T(8,128)(2,1)S(1)} all-gather(bf16[1,12,352]{2,1,0:T(8,128)(2,1)S(1)} %maximum_bitcast_fusion.1), channel_id=1, replica_groups=mesh['role'=2,'dp_0'=4,'dp_1'=4,'mp_0'=4,'mp_1'=2] {'role','dp_0','dp_1'}, dimensions={0}, use_global_device_ids=true | all-gather | bytes 278784 | tf_op jit(solution)/shard_map/all_gather | solution.py:56
  102.9 4.8 all-to-all-start.1
  113.9 11.1 %all-to-all-done.1 = bf16[8,512,160]{1,2,0:T(8,128)(2,1)S(1)} async-done(((bf16[8,512,160]{1,2,0:T(8,128)(2,1)}), bf16[8,512,160]{1,2,0:T(8,128)(2,1)S(1)}, u32[]{:S(2)}, u32[]{:S(2)}) %all-to-all-start.1) | async-done | bytes 1310752 | tf_op jit(solution)/shard_map/all_to_all | solution.py:27
  124.9 32.0 %all-gather.6.cloned.1.call-done = bf16[1280,640]{1,0:T(8,128)(2,1)} async-done(((bf16[40,640]{1,0:T(8,128)(2,1)}), bf16[1280,640]{1,0:T(8,128)(2,1)}) %all-gather.6.cloned.1.call-update) | async-done | bytes 1638416 | tf_op jit(solution)/shard_map/all_gather | solution.py:150
  156.9 142.1 %all-gather.8.cloned.1.call-done = bf16[640,1280]{0,1:T(8,128)(2,1)} async-done(((bf16[640,40]{0,1:T(8,128)(2,1)}), bf16[640,1280]{0,1:T(8,128)(2,1)}) %all-gather.8.cloned.1.call-update) | async-done | bytes 1638416 | tf_op jit(solution)/shard_map/all_gather | solution.py:151
  299.0 8.5 %conditional.1 = (f32[512,1280]{1,0:T(8,128)}) conditional(s32[]{:T(128)} %convert_element_type.101, () %tuple.14, (bf16[512,8,160]{0,2,1:T(8,128)(2,1)S(1)}, bf16[1280,640]{1,0:T(8,128)(2,1)}, bf16[640,1280]{0,1:T(8,128)(2,1)}) %tuple.41), branch_computations={%region_5.0_spmd, %region_6.9_spmd} | conditional | flops 1687224832 | bytes 12470280 | solution.py:163
  301.1 6.4 %fusion.10 = f32[512,1280]{1,0:T(8,128)} fusion(bf16[640,1280]{0,1:T(8,128)(2,1)} %get-tuple-element.25, bf16[512,1280]{0,1:T(8,128)(2,1)} %fusion.1, bf16[1280,640]{1,0:T(8,128)(2,1)} %get-tuple-element.11), kind=kOutput, calls=%fused_computation.14 | convolution fusion | flops 1680670720 | bytes 7208960 | tf_op jit(solution)/shard_map/cond/branch_1_fun/dot_general | solution.py:158
  307.5 3.2 copy.34
  312.0 5.7 all-to-all-start.3
  318.4 7.2 %all-to-all-done.3 = f32[16,1,1]{2,1,0:T(1,128)S(1)} async-done(((f32[16,1,1]{2,1,0:T(1,128)}), f32[16,1,1]{2,1,0:T(1,128)S(1)}, u32[]{:S(2)}, u32[]{:S(2)}) %all-to-all-start.3) | async-done | bytes 96 | tf_op jit(solution)/shard_map/all_to_all | solution.py:27
  329.3 13.2 %reduce-scatter.3.cloned.1.call-done = f32[512,160]{0,1:T(8,128)} async-done(((f32[512,1280]{0,1:T(8,128)}), f32[512,160]{0,1:T(8,128)}) %reduce-scatter.3.cloned.1.call-update) | async-done | bytes 327696 | tf_op jit(solution)/shard_map/reduce_scatter | solution.py:164
  344.2 7.0 %all-to-all-start.2 = ((f32[8,1,1024]{2,1,0:T(1,128)}), f32[8,1,1024]{2,1,0:T(1,128)S(1)}, u32[]{:S(2)}, u32[]{:S(2)}) async-start(f32[8,1,1024]{2,1,0:T(1,128)} %broadcast_in_dim.12), calls=%async_computation.3 | async-start | bytes 65536 | tf_op jit(solution)/shard_map/all_to_all | solution.py:27
  351.2 4.0 all-to-all-done.2
  356.3 7.8 %collective-permute-start = (bf16[512,160]{0,1:T(8,128)(2,1)S(1)}, bf16[512,160]{0,1:T(8,128)(2,1)S(1)}, u32[]{:S(2)}, u32[]{:S(2)}) collective-permute-start(bf16[512,160]{0,1:T(8,128)(2,1)S(1)} %multiply_convert_fusion.2), channel_id=1, source_target_pairs={{0,128},{1,129},{2,130},{3,131},{4,132},{5,133},{6,134},{7,135},{8... | collective-permute-start | bytes 491528 | tf_op jit(solution)/shard_map/ppermute | solution.py:50
  371.0 36.0 %reduce-scatter.5.cloned.1.call-done = f32[128,384]{1,0:T(8,128)} async-done(((f32[1024,384]{1,0:T(8,128)}), f32[128,384]{1,0:T(8,128)}) %reduce-scatter.5.cloned.1.call-update) | async-done | bytes 196624 | tf_op jit(solution)/shard_map/reduce_scatter | solution.py:71
  408.8 27.1 %all-gather.10.cloned.1.call-done = f32[1024,384]{1,0:T(8,128)} async-done(((f32[128,384]{1,0:T(8,128)}), f32[1024,384]{1,0:T(8,128)}) %all-gather.10.cloned.1.call-update) | async-done | bytes 1572880 | tf_op jit(solution)/shard_map/all_gather | solution.py:74
  444.4 10.0 %all-to-all-start.4 = ((f32[32,192,12]{1,2,0:T(8,128)}), f32[32,192,12]{1,2,0:T(8,128)S(1)}, u32[]{:S(2)}, u32[]{:S(2)}) async-start(f32[32,192,12]{1,2,0:T(8,128)} %bitcast.9), calls=%async_computation.6 | async-start | bytes 1048576 | tf_op jit(solution)/shard_map/all_to_all | solution.py:99
  456.4 16.2 %psum.43 = f32[]{:T(128)} all-reduce(f32[]{:T(128)S(6)} %mul.192), channel_id=1, replica_groups=mesh['role'=2,'dp_0'=4,'dp_1'=4,'mp_0'=4,'mp_1'=2] {'role'}, use_global_device_ids=true, to_apply=%region_14.0 | all-reduce | flops 1 | bytes 8 | tf_op jit(solution)/shard_map/psum | solution.py:61
  472.6 10.4 %psum.44 = f32[]{:T(128)} all-reduce(f32[]{:T(128)} %psum.43), channel_id=1, replica_groups=mesh['role'=2,'dp_0'=4,'dp_1'=4,'mp_0'=4,'mp_1'=2] {'dp_0'}, use_global_device_ids=true, to_apply=%region_15.0 | all-reduce | flops 1 | bytes 8 | tf_op jit(solution)/shard_map/psum | solution.py:61
  483.6 10.3 %psum.45 = f32[]{:T(128)} all-reduce(f32[]{:T(128)} %psum.44), channel_id=1, replica_groups=mesh['role'=2,'dp_0'=4,'dp_1'=4,'mp_0'=4,'mp_1'=2] {'dp_1'}, use_global_device_ids=true, to_apply=%region_16.0 | all-reduce | flops 1 | bytes 8 | tf_op jit(solution)/shard_map/psum | solution.py:61
  494.5 10.4 %psum.46 = f32[]{:T(128)} all-reduce(f32[]{:T(128)} %psum.45), channel_id=1, replica_groups=mesh['role'=2,'dp_0'=4,'dp_1'=4,'mp_0'=4,'mp_1'=2] {'mp_0'}, use_global_device_ids=true, to_apply=%region_17.0 | all-reduce | flops 1 | bytes 8 | tf_op jit(solution)/shard_map/psum | solution.py:61
  504.9 3.1 psum.47
  508.6 98.4 %all-reduce.7.cloned.1.call-done = bf16[1280,128]{1,0:T(8,128)(2,1)} async-done(((bf16[1280,128]{1,0:T(8,128)(2,1)}), bf16[1280,128]{1,0:T(8,128)(2,1)}) %all-reduce.7.cloned.1.call-update) | async-done | bytes 327696
  (104 shorter events, 44.5 us)
Async XLA Ops:
  8.0 92.6 %copy-start = (bf16[1568,160]{0,1:T(8,128)(2,1)S(1)}, bf16[1568,160]{0,1:T(8,128)(2,1)}, u32[]{:S(2)}) copy-start(bf16[1568,160]{0,1:T(8,128)(2,1)} %param.12) | copy-start | bytes 1505284
  8.0 91.0 %copy-start.1 = (bf16[1024,384]{1,0:T(8,128)(2,1)S(1)}, bf16[1024,384]{1,0:T(8,128)(2,1)}, u32[]{:S(2)}) copy-start(bf16[1024,384]{1,0:T(8,128)(2,1)} %param.13) | copy-start | bytes 2359300
  8.0 91.7 %copy-start.14 = (s32[1,1024]{1,0:T(1,128)S(1)}, s32[1,1024]{1,0:T(1,128)}, u32[]{:S(2)}) copy-start(s32[1,1024]{1,0:T(1,128)} %param.19) | copy-start | bytes 12292
  8.0 148.9 %all-gather.6.cloned.1.call-start = ((), (), s32[]{:S(2)}) async-start(), calls=%async_computation.8 | async-start | bytes 1689600 | tf_op jit(solution)/shard_map/all_gather | solution.py:150
  8.8 290.2 %all-gather.8.cloned.1.call-start = ((), (), s32[]{:S(2)}) async-start(), calls=%async_computation.9 | async-start | bytes 1689600 | tf_op jit(solution)/shard_map/all_gather | solution.py:151
  10.9 90.7 %all-to-all-start = ((bf16[32,192,12]{1,2,0:T(8,128)(2,1)}), bf16[32,192,12]{1,2,0:T(8,128)(2,1)S(1)}, u32[]{:S(2)}, u32[]{:S(2)}) async-start(bf16[32,192,12]{1,2,0:T(8,128)(2,1)} %broadcast_in_dim.10), calls=%async_computation | async-start | bytes 524288 | tf_op jit(solution)/shard_map/all_to_all | solution.py:27
  102.9 22.0 %all-to-all-start.1 = ((bf16[8,512,160]{1,2,0:T(8,128)(2,1)}), bf16[8,512,160]{1,2,0:T(8,128)(2,1)S(1)}, u32[]{:S(2)}, u32[]{:S(2)}) async-start(bf16[8,512,160]{1,2,0:T(8,128)(2,1)} %broadcast_in_dim.11), calls=%async_computation.1 | async-start | bytes 2621440 | tf_op jit(solution)/shard_map/all_to_all | solution.py:27
  107.7 219.2 %all-reduce.5.cloned.1.call-start = ((), (), s32[]{:S(2)}) async-start(), calls=%async_computation.7 | async-start | bytes 3145728 | tf_op jit(solution)/shard_map/psum | solution.py:194
  109.3 4.5 copy-start.4
  113.8 228.6 %reduce-scatter.3.cloned.1.call-start = ((), (), s32[]{:S(2)}) async-start(), calls=%async_computation.10 | async-start | bytes 2949120 | tf_op jit(solution)/shard_map/reduce_scatter | solution.py:164
  312.0 13.6 %all-to-all-start.3 = ((f32[16,1,1]{2,1,0:T(1,128)}), f32[16,1,1]{2,1,0:T(1,128)S(1)}, u32[]{:S(2)}, u32[]{:S(2)}) async-start(f32[16,1,1]{2,1,0:T(1,128)} %broadcast_in_dim.13), calls=%async_computation.4 | async-start | bytes 16384 | tf_op jit(solution)/shard_map/all_to_all | solution.py:27
  326.8 1.9 copy-start.2
  328.7 13.8 %copy-start.10 = (bf16[512,160]{0,1:T(8,128)(2,1)S(1)}, bf16[512,160]{0,1:T(8,128)(2,1)}, u32[]{:S(2)}) copy-start(bf16[512,160]{0,1:T(8,128)(2,1)} %copy-done.9) | copy-start | bytes 491524
  344.2 11.1 %all-to-all-start.2 = ((f32[8,1,1024]{2,1,0:T(1,128)}), f32[8,1,1024]{2,1,0:T(1,128)S(1)}, u32[]{:S(2)}, u32[]{:S(2)}) async-start(f32[8,1,1024]{2,1,0:T(1,128)} %broadcast_in_dim.12), calls=%async_computation.3 | async-start | bytes 65536 | tf_op jit(solution)/shard_map/all_to_all | solution.py:27
  351.2 55.7 %reduce-scatter.5.cloned.1.call-start = ((), (), s32[]{:S(2)}) async-start(), calls=%async_computation.11 | async-start | bytes 1769472 | tf_op jit(solution)/shard_map/reduce_scatter | solution.py:71
  356.3 11.2 %copy-start.8 = (bf16[384,352]{1,0:T(8,128)(2,1)S(1)}, bf16[384,352]{1,0:T(8,128)(2,1)}, u32[]{:S(2)}) copy-start(bf16[384,352]{1,0:T(8,128)(2,1)} %reshape.189) | copy-start | bytes 811012
  356.3 11.1 %collective-permute-start = (bf16[512,160]{0,1:T(8,128)(2,1)S(1)}, bf16[512,160]{0,1:T(8,128)(2,1)S(1)}, u32[]{:S(2)}, u32[]{:S(2)}) collective-permute-start(bf16[512,160]{0,1:T(8,128)(2,1)S(1)} %multiply_convert_fusion.2), channel_id=1, source_target_pairs={{0,128},{1,129},{2,130},{3,131},{4,132},{5,133},{6,134},{7,135},{8... | collective-permute-start | bytes 491528 | tf_op jit(solution)/shard_map/ppermute | solution.py:50
  364.5 4.5 copy-start.7
  370.7 65.2 %all-gather.10.cloned.1.call-start = ((), (), s32[]{:S(2)}) async-start(), calls=%async_computation.12 | async-start | bytes 1769472 | tf_op jit(solution)/shard_map/all_gather | solution.py:74
  436.0 2.3 copy-start.3
  438.2 1.8 copy-start.5
  444.4 38.6 %copy-start.15 = (u32[256]{0:T(256)S(1)}, u32[256]{0:T(256)}, u32[]{:S(2)}) copy-start(u32[256]{0:T(256)} %constant.79) | copy-start | bytes 3076
  444.4 165.4 %all-to-all-start.4 = ((f32[32,192,12]{1,2,0:T(8,128)}), f32[32,192,12]{1,2,0:T(8,128)S(1)}, u32[]{:S(2)}, u32[]{:S(2)}) async-start(f32[32,192,12]{1,2,0:T(8,128)} %bitcast.9), calls=%async_computation.6 | async-start | bytes 1048576 | tf_op jit(solution)/shard_map/all_to_all | solution.py:99
  454.4 152.7 %all-reduce.7.cloned.1.call-start = ((), (), s32[]{:S(2)}) async-start(), calls=%async_computation.13 | async-start | bytes 655360
  (5 other events, 5.8 us)
Sparse Core Ops, SparseCore 0:
  10.6 146.2 all-gather.5
  158.7 140.2 all-gather.7
  458.6 148.3 all-reduce.6
Sparse Core Ops, SparseCore 1:
  113.9 67.6 all-reduce.4
  310.8 31.6 reduce-scatter.2
  370.8 36.1 reduce-scatter.4
  408.8 27.1 all-gather.9
where the time goes:
time: 620 us; the launch traced here: 619 us
  waiting for transfers between devices  375 us (60%)
  blocking collectives  126 us (20%)
  starting transfers between devices  47.1 us (8%)
  between operations  20.9 us (3%)
  matrix products  19.1 us (3%)
  local copies, waits for them, and re-layouts  15.9 us (3%)
  other arithmetic  14.2 us (2%)
    all_gather x1, waiting for transfers between devices, body(): down_rows = lax.all_gather(ema_down, ROLE_DP, axis=1, tiled=True)  142 us
    unnamed x8, waiting for transfers between devices  99.9 us
    all_gather x1, blocking collectives, sent_together(): filled = lax.all_gather(both, axis, axis=dim, tiled=True)  75.8 us
    psum x5, blocking collectives, by_axis(): return functools.reduce(lax.psum, axes, shard)  50.4 us
    reduce_scatter x1, waiting for transfers between devices, sum_by_parts(): lax.psum_scatter(filled_up(lines, lax.axis_size(axis)), axis, scatter_dim...  36 us
    all_gather x1, waiting for transfers between devices, body(): up_cols = lax.all_gather(ema_up, ROLE_DP, axis=0, tiled=True)  32 us
    all_to_all x4, starting transfers between devices, from_everyone(): return lax.all_to_all(copies, axis, split_axis=0, concat_axis=0, tiled=True)  29 us
    all_gather x1, waiting for transfers between devices, sum_by_parts(): whole = lax.all_gather(own, axis).reshape(-1, *lines.shape[1:])  27.1 us
  transfers between devices with their start and end apart: 13, of which 10 were waited for; matrix products, arithmetic and copies ran while one was open for 6% of the time, Pallas kernels for 0%

commit v1 on v0

--- a/solution.py
+++ b/solution.py
@@ -148,7 +148,9 @@
     working = role_index >= 0
     block_rows = own_rows.shape[0]
     up_cols = lax.all_gather(ema_up, ROLE_DP, axis=0, tiled=True)
-    down_rows = lax.all_gather(ema_down, ROLE_DP, axis=1, tiled=True)
+    down_rows = jnp.concatenate(
+        lax.all_to_all(jnp.stack([ema_down] * lax.axis_size(ROLE_DP)), ROLE_DP, 0, 0), axis=1
+    )
 
     def encode_block():
         normed = normalize(whole_rows.astype(jnp.float32)).astype(jnp.bfloat16)

time: 620 us -> 566 us (0.913)
  waiting for transfers between devices: 375 us -> 280 us
  blocking collectives: 126 us -> 164 us
    all_gather x1 -> x0, waiting for transfers between devices: 142 us -> none  [body(): down_rows = lax.all_gather(ema_down, ROLE_DP, axis=1, tiled=True)]
    all_gather x1, blocking collectives: 75.8 us -> 113 us  [sent_together(): filled = lax.all_gather(both, axis, axis=dim, tiled=True)]
    psum x1, waiting for transfers between devices: 0.03 us -> 34.8 us  [body(): lax.psum(jnp.dot(hid_act, down_cols, preferred_element_type=jnp.float32),...]
    all_gather x1, waiting for transfers between devices: 32 us -> 4.71 us  [body(): up_cols = lax.all_gather(ema_up, ROLE_DP, axis=0, tiled=True)]
    reduce_scatter x1, waiting for transfers between devices: 13.2 us -> 35.9 us  [body(): branch = lax.psum_scatter(partial_sum, MP, scatter_dimension=1, tiled=True)]
    all_to_all x4, waiting for transfers between devices: 22.2 us -> 39.6 us  [from_everyone(): return lax.all_to_all(copies, axis, split_axis=0, concat_axis=0, tiled=True)]
    unnamed x8 -> x7, waiting for transfers between devices: 99.9 us -> 99.2 us
  transfers between devices with their start and end apart: 13 -> 13, of which waited for: 10 -> 11; matrix products, arithmetic and copies ran while one was open for 6% -> 6% of each run, Pallas kernels for 0% -> 0%
where the time goes in v1:
time: 566 us; the launch traced here: 565 us
  waiting for transfers between devices  280 us (49%)
  blocking collectives  164 us (29%)
  starting transfers between devices  50 us (9%)
  between operations  21.1 us (4%)
  local copies, waits for them, and re-layouts  18.2 us (3%)
  matrix products  18.2 us (3%)
  other arithmetic  13.5 us (2%)
    all_gather x1, blocking collectives, sent_together(): filled = lax.all_gather(both, axis, axis=dim, tiled=True)  113 us
    unnamed x7, waiting for transfers between devices  99.2 us
    psum x5, blocking collectives, by_axis(): return functools.reduce(lax.psum, axes, shard)  50.4 us
    all_to_all x4, waiting for transfers between devices, from_everyone(): return lax.all_to_all(copies, axis, split_axis=0, concat_axis=0, tiled=True)  39.6 us
    reduce_scatter x1, waiting for transfers between devices, sum_by_parts(): lax.psum_scatter(filled_up(lines, lax.axis_size(axis)), axis, scatter_dim...  35.9 us
    reduce_scatter x1, waiting for transfers between devices, body(): branch = lax.psum_scatter(partial_sum, MP, scatter_dimension=1, tiled=True)  35.9 us
    psum x1, waiting for transfers between devices, body(): lax.psum(jnp.dot(hid_act, down_cols, preferred_element_type=jnp.float32),...  34.8 us
    all_gather x1, waiting for transfers between devices, sum_by_parts(): whole = lax.all_gather(own, axis).reshape(-1, *lines.shape[1:])  27.1 us
  transfers between devices with their start and end apart: 13, of which 11 were waited for; matrix products, arithmetic and copies ran while one was open for 6% of the time, Pallas kernels for 0%

profile of v1, /device:TPU:2, one launch (start us, length us, event | category | flops | bytes accessed | tf_op | source)
XLA Modules:
  0.0 565.0 jit_solution(11095900421214824863)
XLA Ops:
  9.5 11.5 %all-to-all-start = ((bf16[32,192,12]{1,2,0:T(8,128)(2,1)}), bf16[32,192,12]{1,2,0:T(8,128)(2,1)S(1)}, u32[]{:S(2)}, u32[]{:S(2)}) async-start(bf16[32,192,12]{1,2,0:T(8,128)(2,1)} %broadcast_in_dim.10), calls=%async_computation | async-start | bytes 524288 | tf_op jit(solution)/shard_map/all_to_all | solution.py:27
  22.6 12.0 %all-to-all-done = bf16[32,192,12]{1,2,0:T(8,128)(2,1)S(1)} async-done(((bf16[32,192,12]{1,2,0:T(8,128)(2,1)}), bf16[32,192,12]{1,2,0:T(8,128)(2,1)S(1)}, u32[]{:S(2)}, u32[]{:S(2)}) %all-to-all-start) | async-done | bytes 147488 | tf_op jit(solution)/shard_map/all_to_all | solution.py:27
  35.8 5.0 all-to-all-start.1
  41.5 16.6 %all-to-all-done.1 = bf16[8,512,160]{1,2,0:T(8,128)(2,1)S(1)} async-done(((bf16[8,512,160]{1,2,0:T(8,128)(2,1)}), bf16[8,512,160]{1,2,0:T(8,128)(2,1)S(1)}, u32[]{:S(2)}, u32[]{:S(2)}) %all-to-all-start.1) | async-done | bytes 1310752 | tf_op jit(solution)/shard_map/all_to_all | solution.py:27
  59.4 4.8 all-to-all-start.2
  64.4 113.4 %all-gather.1 = bf16[32,12,352]{2,1,0:T(8,128)(2,1)S(1)} all-gather(bf16[1,12,352]{2,1,0:T(8,128)(2,1)S(1)} %maximum_bitcast_fusion.1), channel_id=1, replica_groups=mesh['role'=2,'dp_0'=4,'dp_1'=4,'mp_0'=4,'mp_1'=2] {'role','dp_0','dp_1'}, dimensions={0}, use_global_device_ids=true | all-gather | bytes 278784 | tf_op jit(solution)/shard_map/all_gather | solution.py:56
  184.9 4.7 all-gather.5.cloned.1.call-done
  189.6 8.5 %conditional.1 = (f32[512,1280]{1,0:T(8,128)}) conditional(s32[]{:T(128)} %convert_element_type.101, () %tuple.14, (bf16[512,8,160]{0,2,1:T(8,128)(2,1)S(1)}, bf16[1280,640]{1,0:T(8,128)(2,1)}, bf16[640,32,40]{0,2,1:T(8,128)(2,1)}) %tuple.36), branch_computations={%region_5.0_spmd, %region_6.9_spmd} | conditional | flops 1687224832 | bytes 12470280 | solution.py:165
  191.7 6.4 %fusion.10 = f32[512,1280]{1,0:T(8,128)} fusion(bf16[640,1280]{0,1:T(8,128)(2,1)} %bitcast.1, bf16[512,1280]{0,1:T(8,128)(2,1)} %fusion.1, bf16[1280,640]{1,0:T(8,128)(2,1)} %get-tuple-element.12), kind=kOutput, calls=%fused_computation.14 | convolution fusion | flops 1680670720 | bytes 7208960 | tf_op jit(solution)/shard_map/cond/branch_1_fun/dot_general | solution.py:160
  202.7 3.5 all-to-all-start.4
  206.8 7.1 %all-to-all-done.4 = f32[16,1,1]{2,1,0:T(1,128)S(1)} async-done(((f32[16,1,1]{2,1,0:T(1,128)}), f32[16,1,1]{2,1,0:T(1,128)S(1)}, u32[]{:S(2)}, u32[]{:S(2)}) %all-to-all-start.4) | async-done | bytes 96 | tf_op jit(solution)/shard_map/all_to_all | solution.py:27
  215.2 34.8 %all-reduce.5.cloned.1.call-done = f32[1024,384]{1,0:T(8,128)} async-done(((f32[1024,384]{1,0:T(8,128)}), f32[1024,384]{1,0:T(8,128)}) %all-reduce.5.cloned.1.call-update) | async-done | bytes 1572880 | tf_op jit(solution)/shard_map/psum | solution.py:196
  252.4 35.9 %reduce-scatter.3.cloned.1.call-done = f32[512,160]{0,1:T(8,128)} async-done(((f32[512,1280]{0,1:T(8,128)}), f32[512,160]{0,1:T(8,128)}) %reduce-scatter.3.cloned.1.call-update) | async-done | bytes 327696 | tf_op jit(solution)/shard_map/reduce_scatter | solution.py:166
  290.0 7.1 %all-to-all-start.3 = ((f32[8,1,1024]{2,1,0:T(1,128)}), f32[8,1,1024]{2,1,0:T(1,128)S(1)}, u32[]{:S(2)}, u32[]{:S(2)}) async-start(f32[8,1,1024]{2,1,0:T(1,128)} %broadcast_in_dim.12), calls=%async_computation.4 | async-start | bytes 65536 | tf_op jit(solution)/shard_map/all_to_all | solution.py:27
  297.1 4.0 all-to-all-done.3
  302.2 7.8 %collective-permute-start = (bf16[512,160]{0,1:T(8,128)(2,1)S(1)}, bf16[512,160]{0,1:T(8,128)(2,1)S(1)}, u32[]{:S(2)}, u32[]{:S(2)}) collective-permute-start(bf16[512,160]{0,1:T(8,128)(2,1)S(1)} %multiply_convert_fusion.2), channel_id=1, source_target_pairs={{0,128},{1,129},{2,130},{3,131},{4,132},{5,133},{6,134},{7,135},{8... | collective-permute-start | bytes 491528 | tf_op jit(solution)/shard_map/ppermute | solution.py:50
  316.8 35.9 %reduce-scatter.5.cloned.1.call-done = f32[128,384]{1,0:T(8,128)} async-done(((f32[1024,384]{1,0:T(8,128)}), f32[128,384]{1,0:T(8,128)}) %reduce-scatter.5.cloned.1.call-update) | async-done | bytes 196624 | tf_op jit(solution)/shard_map/reduce_scatter | solution.py:71
  354.6 27.1 %all-gather.7.cloned.1.call-done = f32[1024,384]{1,0:T(8,128)} async-done(((f32[128,384]{1,0:T(8,128)}), f32[1024,384]{1,0:T(8,128)}) %all-gather.7.cloned.1.call-update) | async-done | bytes 1572880 | tf_op jit(solution)/shard_map/all_gather | solution.py:74
  390.2 10.0 %all-to-all-start.5 = ((f32[32,192,12]{1,2,0:T(8,128)}), f32[32,192,12]{1,2,0:T(8,128)S(1)}, u32[]{:S(2)}, u32[]{:S(2)}) async-start(f32[32,192,12]{1,2,0:T(8,128)} %bitcast.11), calls=%async_computation.7 | async-start | bytes 1048576 | tf_op jit(solution)/shard_map/all_to_all | solution.py:99
  402.1 16.2 %psum.43 = f32[]{:T(128)} all-reduce(f32[]{:T(128)S(6)} %mul.192), channel_id=1, replica_groups=mesh['role'=2,'dp_0'=4,'dp_1'=4,'mp_0'=4,'mp_1'=2] {'role'}, use_global_device_ids=true, to_apply=%region_14.0 | all-reduce | flops 1 | bytes 8 | tf_op jit(solution)/shard_map/psum | solution.py:61
  418.4 10.4 %psum.44 = f32[]{:T(128)} all-reduce(f32[]{:T(128)} %psum.43), channel_id=1, replica_groups=mesh['role'=2,'dp_0'=4,'dp_1'=4,'mp_0'=4,'mp_1'=2] {'dp_0'}, use_global_device_ids=true, to_apply=%region_15.0 | all-reduce | flops 1 | bytes 8 | tf_op jit(solution)/shard_map/psum | solution.py:61
  429.4 10.3 %psum.45 = f32[]{:T(128)} all-reduce(f32[]{:T(128)} %psum.44), channel_id=1, replica_groups=mesh['role'=2,'dp_0'=4,'dp_1'=4,'mp_0'=4,'mp_1'=2] {'dp_1'}, use_global_device_ids=true, to_apply=%region_16.0 | all-reduce | flops 1 | bytes 8 | tf_op jit(solution)/shard_map/psum | solution.py:61
  440.3 10.4 %psum.46 = f32[]{:T(128)} all-reduce(f32[]{:T(128)} %psum.45), channel_id=1, replica_groups=mesh['role'=2,'dp_0'=4,'dp_1'=4,'mp_0'=4,'mp_1'=2] {'mp_0'}, use_global_device_ids=true, to_apply=%region_17.0 | all-reduce | flops 1 | bytes 8 | tf_op jit(solution)/shard_map/psum | solution.py:61
  454.4 98.4 %all-reduce.7.cloned.1.call-done = bf16[1280,128]{1,0:T(8,128)(2,1)} async-done(((bf16[1280,128]{1,0:T(8,128)(2,1)}), bf16[1280,128]{1,0:T(8,128)(2,1)}) %all-reduce.7.cloned.1.call-update) | async-done | bytes 327696
  (110 shorter events, 50.7 us)
Async XLA Ops:
  8.0 13.7 %copy-start = (bf16[1568,160]{0,1:T(8,128)(2,1)S(1)}, bf16[1568,160]{0,1:T(8,128)(2,1)}, u32[]{:S(2)}) copy-start(bf16[1568,160]{0,1:T(8,128)(2,1)} %param.12) | copy-start | bytes 1505284
  9.5 25.1 %all-to-all-start = ((bf16[32,192,12]{1,2,0:T(8,128)(2,1)}), bf16[32,192,12]{1,2,0:T(8,128)(2,1)S(1)}, u32[]{:S(2)}, u32[]{:S(2)}) async-start(bf16[32,192,12]{1,2,0:T(8,128)(2,1)} %broadcast_in_dim.10), calls=%async_computation | async-start | bytes 524288 | tf_op jit(solution)/shard_map/all_to_all | solution.py:27
  22.6 13.2 %copy-start.10 = (bf16[512,160]{0,1:T(8,128)(2,1)}, bf16[512,160]{0,1:T(8,128)(2,1)S(1)}, u32[]{:S(2)}) copy-start(bf16[512,160]{0,1:T(8,128)(2,1)S(1)} %fusion.29) | copy-start | bytes 491524
  35.8 22.3 %copy-start.15 = (bf16[640,40]{0,1:T(8,128)(2,1)S(1)}, bf16[640,40]{0,1:T(8,128)(2,1)}, u32[]{:S(2)}) copy-start(bf16[640,40]{0,1:T(8,128)(2,1)} %param.15) | copy-start | bytes 153604
  35.8 22.2 %all-to-all-start.1 = ((bf16[8,512,160]{1,2,0:T(8,128)(2,1)}), bf16[8,512,160]{1,2,0:T(8,128)(2,1)S(1)}, u32[]{:S(2)}, u32[]{:S(2)}) async-start(bf16[8,512,160]{1,2,0:T(8,128)(2,1)} %broadcast_in_dim.11), calls=%async_computation.1 | async-start | bytes 2621440 | tf_op jit(solution)/shard_map/all_to_all | solution.py:27
  40.7 148.9 %all-gather.5.cloned.1.call-start = ((), (), s32[]{:S(2)}) async-start(), calls=%async_computation.9 | async-start | bytes 1689600 | tf_op jit(solution)/shard_map/all_gather | solution.py:150
  59.4 4.9 copy-start.16
  59.4 4.9 copy-start.17
  59.4 119.2 %copy-start.1 = (bf16[1024,384]{1,0:T(8,128)(2,1)S(1)}, bf16[1024,384]{1,0:T(8,128)(2,1)}, u32[]{:S(2)}) copy-start(bf16[1024,384]{1,0:T(8,128)(2,1)} %param.13) | copy-start | bytes 2359300
  59.4 125.5 %all-to-all-start.2 = ((bf16[32,640,40]{1,2,0:T(8,128)(2,1)}), bf16[32,640,40]{1,2,0:T(8,128)(2,1)}, u32[]{:S(2)}, u32[]{:S(2)}) async-start(bf16[32,640,40]{1,2,0:T(8,128)(2,1)} %stack.2), calls=%async_computation.2 | async-start | bytes 3276800 | tf_op jit(solution)/shard_map/all_to_all | solution.py:152
  64.2 185.8 %all-reduce.5.cloned.1.call-start = ((), (), s32[]{:S(2)}) async-start(), calls=%async_computation.8 | async-start | bytes 3145728 | tf_op jit(solution)/shard_map/psum | solution.py:196
  180.3 4.5 copy-start.4
  184.8 103.4 %reduce-scatter.3.cloned.1.call-start = ((), (), s32[]{:S(2)}) async-start(), calls=%async_computation.10 | async-start | bytes 2949120 | tf_op jit(solution)/shard_map/reduce_scatter | solution.py:166
  202.7 11.3 %all-to-all-start.4 = ((f32[16,1,1]{2,1,0:T(1,128)}), f32[16,1,1]{2,1,0:T(1,128)S(1)}, u32[]{:S(2)}, u32[]{:S(2)}) async-start(f32[16,1,1]{2,1,0:T(1,128)} %broadcast_in_dim.13), calls=%async_computation.5 | async-start | bytes 16384 | tf_op jit(solution)/shard_map/all_to_all | solution.py:27
  251.8 36.5 %copy-start.11 = (bf16[512,160]{0,1:T(8,128)(2,1)S(1)}, bf16[512,160]{0,1:T(8,128)(2,1)}, u32[]{:S(2)}) copy-start(bf16[512,160]{0,1:T(8,128)(2,1)} %copy-done.10) | copy-start | bytes 491524
  290.0 11.1 %all-to-all-start.3 = ((f32[8,1,1024]{2,1,0:T(1,128)}), f32[8,1,1024]{2,1,0:T(1,128)S(1)}, u32[]{:S(2)}, u32[]{:S(2)}) async-start(f32[8,1,1024]{2,1,0:T(1,128)} %broadcast_in_dim.12), calls=%async_computation.4 | async-start | bytes 65536 | tf_op jit(solution)/shard_map/all_to_all | solution.py:27
  297.1 55.7 %reduce-scatter.5.cloned.1.call-start = ((), (), s32[]{:S(2)}) async-start(), calls=%async_computation.11 | async-start | bytes 1769472 | tf_op jit(solution)/shard_map/reduce_scatter | solution.py:71
  302.2 11.2 %copy-start.9 = (bf16[384,352]{1,0:T(8,128)(2,1)S(1)}, bf16[384,352]{1,0:T(8,128)(2,1)}, u32[]{:S(2)}) copy-start(bf16[384,352]{1,0:T(8,128)(2,1)} %reshape.199) | copy-start | bytes 811012
  302.2 11.2 %collective-permute-start = (bf16[512,160]{0,1:T(8,128)(2,1)S(1)}, bf16[512,160]{0,1:T(8,128)(2,1)S(1)}, u32[]{:S(2)}, u32[]{:S(2)}) collective-permute-start(bf16[512,160]{0,1:T(8,128)(2,1)S(1)} %multiply_convert_fusion.2), channel_id=1, source_target_pairs={{0,128},{1,129},{2,130},{3,131},{4,132},{5,133},{6,134},{7,135},{8... | collective-permute-start | bytes 491528 | tf_op jit(solution)/shard_map/ppermute | solution.py:50
  310.3 4.5 copy-start.7
  316.6 65.2 %all-gather.7.cloned.1.call-start = ((), (), s32[]{:S(2)}) async-start(), calls=%async_computation.12 | async-start | bytes 1769472 | tf_op jit(solution)/shard_map/all_gather | solution.py:74
  390.2 38.6 %copy-start.18 = (u32[256]{0:T(256)S(1)}, u32[256]{0:T(256)}, u32[]{:S(2)}) copy-start(u32[256]{0:T(256)} %constant.79) | copy-start | bytes 3076
  390.2 165.5 %all-to-all-start.5 = ((f32[32,192,12]{1,2,0:T(8,128)}), f32[32,192,12]{1,2,0:T(8,128)S(1)}, u32[]{:S(2)}, u32[]{:S(2)}) async-start(f32[32,192,12]{1,2,0:T(8,128)} %bitcast.11), calls=%async_computation.7 | async-start | bytes 1048576 | tf_op jit(solution)/shard_map/all_to_all | solution.py:99
  400.2 152.7 %all-reduce.7.cloned.1.call-start = ((), (), s32[]{:S(2)}) async-start(), calls=%async_computation.13 | async-start | bytes 655360
  (8 other events, 11.4 us)
Sparse Core Ops, SparseCore 0:
  43.3 146.2 all-gather.4
  404.4 148.3 all-reduce.6
Sparse Core Ops, SparseCore 1:
  184.9 65.0 all-reduce.4
  252.4 35.8 reduce-scatter.2
  316.7 36.0 reduce-scatter.4
  354.6 27.1 all-gather.6
